TPU v7x, 512 devices: a whole 4x8x8 slice. The times are simulated.
512 devices in a mesh: grp: 16 (over x, y_hi), dev: 32 (over y_lo, z, core).
Axes of the slice: x: 4, y: 8 (y_hi: 4, y_lo: 2; y = y_hi * 2 + y_lo), z: 8, core: 2. Of those that a mesh axis runs over, the one named last changes fastest.
Arguments:
- raw: bfloat16 [8192, 16, 4096], P(('grp', 'dev'))
- dark: bfloat16 [16, 4096], replicated, may hold values from 0.049804688 to 0.29882812
- basis: bfloat16 [8, 4096], replicated, may hold values from -3 to 3
- counts: int32 [8192], P(('grp', 'dev')), may hold values from 1 to 16, as said below
- positions: int32 [8192], replicated, may hold values from 0 to 8191, as said below
Outputs:
- corrected: bfloat16 [8192, 16, 4096], P(('grp', 'dev'))
- pooled: bfloat16 [16, 16, 1, 491520], P('grp', None, None, 'dev')
Inputs may be any that keep to these rules, and one draw needn't show every extreme that they name: `counts`: the first tile of every device (16 tiles in acquisition order) has all 16 planes. A permutation of the tile positions of the slide image. The 16 tiles of the device at grp index g and dev index d lie in 16 different bands, all at tile columns d * 16 to d * 16 + 15.
All inputs are finite; a program needn't handle non-finite values.
Results may differ from a plain program's by a relative error of at most 0.0046.
Values may be sent and summed in bfloat16 or wider, within the bound.
No kernel may reach another device: no remote copies, remote signals or barrier semaphores. Data moves between devices by JAX's collectives and lax.ppermute only.
A program may use at most 128 MiB of HBM per device.

v0:
```python
import functools

import jax
import jax.numpy as jnp
from jax import lax
from jax.sharding import Mesh
from jax.sharding import PartitionSpec as P

ROWS = 2
COLS = 2048
OVL = 128
GRP = ("grp_0", "grp_1")
DEV = ("dev_0", "dev_1", "dev_2")
GRP_DEV = ("grp_0", "grp_1", "dev_0", "dev_1", "dev_2")


def one_axis_at_a_time(x, axes):
    return functools.reduce(lax.psum, axes, x)


def shifted(value, axis, steps):
    count = lax.axis_size(axis)
    first, last = (max(0, -steps), min(count, count - steps))
    return lax.ppermute(value, axis, [(source, source + steps) for source in range(first, last)])


def feather():
    column = jnp.arange(COLS, dtype=jnp.float32) + 0.5
    return jnp.minimum(1.0, jnp.minimum(column / OVL, (COLS - column) / OVL))


def pooling(tiles):
    count = tiles.shape[0]
    planes = tiles.shape[1]
    shaped = tiles.reshape(count, planes, ROWS, COLS) * feather()
    return jnp.sum(shaped.reshape(count, planes, ROWS // 2, 2, COLS // 2, 2), axis=(3, 5)) * 0.25


def per_device(raw, dark, basis, counts, positions):
    tile_count, planes, pixels = raw.shape
    groups = lax.axis_size(GRP)
    columns = lax.axis_size(DEV)
    band_size = columns * tile_count
    live = (jnp.arange(planes, dtype=jnp.int32)[None, :] < counts[:, None]).astype(jnp.float32)
    projected = jnp.einsum("kx,tpx->tkp", basis, raw, preferred_element_type=jnp.float32)
    local_proj = jnp.sum(projected * live[:, None, :], axis=0)
    ones_row = jnp.ones((pixels,), jnp.bfloat16)
    local_sum = jnp.sum(
        jnp.einsum("tpx,x->tp", raw, ones_row, preferred_element_type=jnp.float32) * live, axis=0
    )
    local_live = jnp.sum(live, axis=0)
    proj, total, alive = (
        one_axis_at_a_time(local_proj, GRP_DEV),
        one_axis_at_a_time(local_sum, GRP_DEV),
        one_axis_at_a_time(local_live, GRP_DEV),
    )
    dark_f = dark.astype(jnp.float32)
    dark_proj = jnp.dot(basis, dark.T, preferred_element_type=jnp.float32)
    dark_sum = jnp.sum(dark_f, axis=1)
    coef = (proj - alive[None, :] * dark_proj) / (total - alive * dark_sum)[None, :]
    shade = jnp.dot(coef.T, basis.astype(jnp.float32), precision=lax.Precision.HIGHEST)
    inverse = jnp.exp(-shade)
    corrected = (
        (raw.astype(jnp.float32) - dark_f[None]) * inverse[None] * live[:, :, None]
    ).astype(jnp.bfloat16)
    here_grp = lax.axis_index(GRP)
    here_dev = lax.axis_index(DEV)
    layout = positions.reshape(groups, columns, tile_count)
    mine = lax.dynamic_index_in_dim(
        lax.dynamic_index_in_dim(layout, here_grp, 0, False), here_dev, 0, False
    )
    select = mine[None, :] // band_size == jnp.arange(groups, dtype=jnp.int32)[:, None]
    column_tiles = lax.dynamic_index_in_dim(layout, here_dev, 1, False)
    arrives = column_tiles // band_size == here_grp
    slot_of = jnp.sum(jnp.where(arrives, column_tiles % tile_count, 0), axis=1)
    place = slot_of[None, :] == jnp.arange(tile_count, dtype=jnp.int32)[:, None]
    own_cells = (
        pooling(corrected.astype(jnp.float32))
        .astype(jnp.bfloat16)
        .reshape(tile_count, planes, ROWS // 2 * (COLS // 2))
    )
    outgoing = jnp.einsum(
        "bs,spx->bpx", select.astype(jnp.bfloat16), own_cells, preferred_element_type=jnp.float32
    ).astype(jnp.bfloat16)
    arrived = lax.all_to_all(outgoing, GRP, split_axis=0, concat_axis=0, tiled=True)
    placed = jnp.einsum(
        "jb,bpx->jpx", place.astype(jnp.bfloat16), arrived, preferred_element_type=jnp.float32
    ).astype(jnp.bfloat16)
    cells = placed.reshape(tile_count, planes, ROWS // 2, COLS // 2)
    cells = lax.optimization_barrier(cells)
    half_step = (COLS - OVL) // 2
    half_ovl = OVL // 2
    head = cells[..., :half_step].astype(jnp.float32)
    tail = cells[..., half_step:]
    spill = shifted(tail[-1], DEV, 1)
    carried = jnp.concatenate([spill[None], tail[:-1]], axis=0)
    carried = jnp.pad(carried, ((0, 0), (0, 0), (0, 0), (0, half_step - half_ovl))).astype(
        jnp.float32
    )
    merged = head + carried
    result = jnp.transpose(merged, (1, 2, 0, 3)).reshape(
        1, planes, ROWS // 2, tile_count * half_step
    )
    return (corrected, result.astype(jnp.bfloat16))


def solution(mesh):
    split = Mesh(mesh.devices.reshape(4, 4, 2, 8, 2), ("grp_0", "grp_1", "dev_0", "dev_1", "dev_2"))
    placed = (P(GRP_DEV, None, None), P(), P(), P(GRP_DEV), P())
    return jax.shard_map(
        per_device,
        mesh=split,
        in_specs=placed,
        out_specs=(P(GRP_DEV, None, None), P(GRP, None, None, DEV)),
        check_vma=False,
    )
```

profile of v0, /device:TPU:8, one launch (start us, length us, event | category | flops | bytes accessed | tf_op | source)
XLA Modules:
  0.0 142.2 jit_solution(6325698254589569034)
XLA Ops:
  0.6 0.0 copy-start
  0.6 0.0 copy-start.2
  0.7 0.0 copy-start.1
  0.7 1.2 convert_reduce_fusion
  1.9 0.9 convert_element_type.62
  2.8 0.7 fusion.18
  3.6 4.1 %fusion.16 = f32[1,16,16]{2,0,1:T(1,128)S(1)} fusion(bf16[16,16,4096]{2,1,0:T(8,128)(2,1)} %param.5), kind=kOutput, calls=%fused_computation.33 | convolution fusion | flops 2097152 | bytes 2098176 | tf_op jit(solution)/shard_map/tpx,x->tp/dot_general | solution.py:49
  7.7 0.8 fusion.27
  8.4 0.0 copy-done
  8.4 4.1 %fusion.2 = f32[16,8]{0,1:T(8,128)S(1)} fusion(bf16[16,16,4096]{2,1,0:T(8,128)(2,1)} %param.5, bf16[8,4096]{1,0:T(8,128)(2,1)S(1)} %copy-done, f32[16,16]{1,0:T(8,128)S(1)} %fusion.18), kind=kOutput, calls=%fused_computation.8 | convolution fusion | flops 16781184 | bytes 2164224 | tf_op jit(solution)/shard_map/kx,tpx->tkp/dot_general | solution.py:45
  12.6 10.6 %all-reduce.3 = (f32[8,16]{1,0:T(8,128)S(1)}, f32[16]{0:T(128)S(1)}, f32[16]{0:T(128)S(1)}) all-reduce(f32[8,16]{1,0:T(8,128)S(1)} %bitcast.43, f32[16]{0:T(128)S(1)} %get-tuple-element.3, f32[16]{0:T(128)S(1)} %get-tuple-element.2), channel_id=1, replica_groups=mesh['grp_0'=4,'grp_1'=4,'dev_0'=2,'dev_1'=8,'dev_2'=2] {'grp_0'}, use_global_device_ids=true, to_apply=%region_1.0 | all-reduce | flops 160 | bytes 1280 | tf_op jit(solution)/shard_map/psum | solution.py:18
  23.2 12.1 %all-reduce.2 = (f32[8,16]{1,0:T(8,128)S(1)}, f32[16]{0:T(128)S(1)}, f32[16]{0:T(128)S(1)}) all-reduce(f32[8,16]{1,0:T(8,128)S(1)} %get-tuple-element.10, f32[16]{0:T(128)S(1)} %get-tuple-element.11, f32[16]{0:T(128)S(1)} %get-tuple-element.12), channel_id=1, replica_groups=mesh['grp_0'=4,'grp_1'=4,'dev_0'=2,'dev_1'=8,'dev_2'=2] {'grp_1'}, use_global_device_ids=true, to_apply=%region_2.0 | all-reduce | flops 160 | bytes 1280 | tf_op jit(solution)/shard_map/psum | solution.py:18
  35.3 5.0 %all-reduce.5 = (f32[8,16]{1,0:T(8,128)S(1)}, f32[16]{0:T(128)S(1)}, f32[16]{0:T(128)S(1)}) all-reduce(f32[8,16]{1,0:T(8,128)S(1)} %get-tuple-element.7, f32[16]{0:T(128)S(1)} %get-tuple-element.8, f32[16]{0:T(128)S(1)} %get-tuple-element.9), channel_id=1, replica_groups=mesh['grp_0'=4,'grp_1'=4,'dev_0'=2,'dev_1'=8,'dev_2'=2] {'dev_0'}, use_global_device_ids=true, to_apply=%region_3.0 | all-reduce | flops 160 | bytes 1280 | tf_op jit(solution)/shard_map/psum | solution.py:18
  40.3 23.4 %all-reduce.1 = (f32[8,16]{1,0:T(8,128)S(1)}, f32[16]{0:T(128)S(1)}, f32[16]{0:T(128)S(1)}) all-reduce(f32[8,16]{1,0:T(8,128)S(1)} %get-tuple-element.16, f32[16]{0:T(128)S(1)} %get-tuple-element.17, f32[16]{0:T(128)S(1)} %get-tuple-element.18), channel_id=1, replica_groups=mesh['grp_0'=4,'grp_1'=4,'dev_0'=2,'dev_1'=8,'dev_2'=2] {'dev_1'}, use_global_device_ids=true, to_apply=%region_4.0 | all-reduce | flops 160 | bytes 1280 | tf_op jit(solution)/shard_map/psum | solution.py:18
  63.7 2.5 %all-reduce.4 = (f32[8,16]{1,0:T(8,128)S(1)}, f32[16]{0:T(128)S(1)}, f32[16]{0:T(128)S(1)}) all-reduce(f32[8,16]{1,0:T(8,128)S(1)} %get-tuple-element.4, f32[16]{0:T(128)S(1)} %get-tuple-element.5, f32[16]{0:T(128)S(1)} %get-tuple-element.6), channel_id=1, replica_groups=mesh['grp_0'=4,'grp_1'=4,'dev_0'=2,'dev_1'=8,'dev_2'=2] {'dev_2'}, use_global_device_ids=true, to_apply=%region_5.0 | all-reduce | flops 160 | bytes 1280 | tf_op jit(solution)/shard_map/psum | solution.py:18
  66.2 0.0 copy-done.2
  66.2 0.1 fusion.4
  66.3 0.3 fusion
  66.7 0.0 copy-done.1
  66.7 2.0 %multiply_convert_fusion = bf16[16,16,4096]{2,1,0:T(8,128)(2,1)} fusion(bf16[16,16,4096]{2,1,0:T(8,128)(2,1)S(1)} %copy-done.1, f32[16,16]{1,0:T(8,128)S(1)} %fusion.18, f32[16,4096]{1,0:T(8,128)S(1)} %fusion, f32[16,4096]{1,0:T(8,128)S(1)} %convert_element_type.62), kind=kLoop, calls=%fused_computation.3 | loop fusion | flops 5242880 | bytes 4719616 | tf_op jit(solution)/shard_map/convert_element_type | solution.py:65
  68.7 16.9 %copy.17 = f32[16,16,4096]{1,0,2:T(8,128)} copy(bf16[16,16,4096]{2,1,0:T(8,128)(2,1)} %multiply_convert_fusion) | data formatting | bytes 6291456 | tf_op jit(solution)/shard_map/reshape | solution.py:35
  85.6 0.2 copy.18
  85.8 16.5 %multiply_reduce_fusion = f32[16,16,1024]{1,0,2:T(8,128)} fusion(f32[16,16,1,2,1024,2]{1,0,5,4,3,2:T(8,128)} %bitcast.40, f32[1024,2]{1,0:T(8,128)S(1)} %copy.18), kind=kLoop, calls=%fused_computation | loop fusion | flops 1835008 | bytes 5251072 | tf_op jit(solution)/shard_map/reduce_sum | solution.py:36
  102.4 0.0 copy-start.3
  102.4 5.1 %copy.19 = f32[16,16,1024]{2,1,0:T(8,128)S(1)} copy(f32[16,16,1024]{1,0,2:T(8,128)} %multiply_reduce_fusion) | data formatting | bytes 2097152 | tf_op jit(solution)/shard_map/reduce_sum | solution.py:36
  107.5 0.1 multiply_convert_fusion.1
  107.6 0.0 copy-done.3
  107.6 0.1 reshape.162
  107.8 0.5 convolution_convert_fusion.1
  108.3 1.1 copy.21
  109.3 4.5 %all-to-all-start = ((bf16[16,16,1024]{2,1,0:T(8,128)(2,1)}), bf16[16,16,1024]{2,1,0:T(8,128)(2,1)S(1)}, u32[]{:S(2)}, u32[]{:S(2)}) async-start(bf16[16,16,1024]{2,1,0:T(8,128)(2,1)} %copy.21), calls=%async_computation | async-start | bytes 1048576 | tf_op jit(solution)/shard_map/all_to_all | solution.py:85
  113.9 0.1 fusion.15
  114.0 19.1 %all-to-all-done = bf16[16,16,1024]{2,1,0:T(8,128)(2,1)S(1)} async-done(((bf16[16,16,1024]{2,1,0:T(8,128)(2,1)}), bf16[16,16,1024]{2,1,0:T(8,128)(2,1)S(1)}, u32[]{:S(2)}, u32[]{:S(2)}) %all-to-all-start) | async-done | bytes 524320 | tf_op jit(solution)/shard_map/all_to_all | solution.py:85
  133.1 0.5 fusion.1
  133.6 0.1 slice.16
  133.7 1.9 %collective-permute-start = (bf16[16,1,64]{2,0,1:T(8,128)(2,1)S(1)}, bf16[16,1,64]{2,0,1:T(8,128)(2,1)S(1)}, u32[]{:S(2)}, u32[]{:S(2)}) collective-permute-start(bf16[16,1,64]{2,0,1:T(8,128)(2,1)S(1)} %bitcast.44), channel_id=1, source_target_pairs={{0,1},{1,2},{2,3},{3,4},{4,5},{5,6},{6,7},{7,8},{8,9},{9,10},{10,1... | collective-permute-start | bytes 6152 | tf_op jit(solution)/shard_map/ppermute | solution.py:24
  135.6 0.1 slice.17
  135.7 5.0 %collective-permute-done = bf16[16,1,64]{2,0,1:T(8,128)(2,1)S(1)} collective-permute-done((bf16[16,1,64]{2,0,1:T(8,128)(2,1)S(1)}, bf16[16,1,64]{2,0,1:T(8,128)(2,1)S(1)}, u32[]{:S(2)}, u32[]{:S(2)}) %collective-permute-start) | collective-permute-done | bytes 2080 | tf_op jit(solution)/shard_map/ppermute | solution.py:24
  140.7 0.1 fusion.7
  140.8 1.4 %convert_element_type.72 = bf16[1,16,1,15360]{3,1,2,0:T(8,128)(2,1)} reshape(bf16[16,1,16,960]{3,2,0,1:T(8,128)(2,1)S(1)} %fusion.7) | data formatting | bytes 983040 | tf_op jit(solution)/shard_map/convert_element_type | solution.py:104
  (6 shorter events, 0.1 us)
Async XLA Ops:
  0.6 7.8 %copy-start = (bf16[8,4096]{1,0:T(8,128)(2,1)S(1)}, bf16[8,4096]{1,0:T(8,128)(2,1)}, u32[]{:S(2)}) copy-start(bf16[8,4096]{1,0:T(8,128)(2,1)} %param.7) | copy-start | bytes 196612
  0.6 65.5 %copy-start.2 = (bf16[16,4096]{1,0:T(8,128)(2,1)S(1)}, bf16[16,4096]{1,0:T(8,128)(2,1)}, u32[]{:S(2)}) copy-start(bf16[16,4096]{1,0:T(8,128)(2,1)} %param.6) | copy-start | bytes 393220
  0.7 66.0 %copy-start.1 = (bf16[16,16,4096]{2,1,0:T(8,128)(2,1)S(1)}, bf16[16,16,4096]{2,1,0:T(8,128)(2,1)}, u32[]{:S(2)}) copy-start(bf16[16,16,4096]{2,1,0:T(8,128)(2,1)} %param.5) | copy-start | bytes 6291460
  102.4 5.2 %copy-start.3 = (s32[8192]{0:T(1024)S(1)}, s32[8192]{0:T(1024)}, u32[]{:S(2)}) copy-start(s32[8192]{0:T(1024)} %param.9) | copy-start | bytes 98308
  109.3 23.8 %all-to-all-start = ((bf16[16,16,1024]{2,1,0:T(8,128)(2,1)}), bf16[16,16,1024]{2,1,0:T(8,128)(2,1)S(1)}, u32[]{:S(2)}, u32[]{:S(2)}) async-start(bf16[16,16,1024]{2,1,0:T(8,128)(2,1)} %copy.21), calls=%async_computation | async-start | bytes 1048576 | tf_op jit(solution)/shard_map/all_to_all | solution.py:85
  133.7 7.0 %collective-permute-start = (bf16[16,1,64]{2,0,1:T(8,128)(2,1)S(1)}, bf16[16,1,64]{2,0,1:T(8,128)(2,1)S(1)}, u32[]{:S(2)}, u32[]{:S(2)}) collective-permute-start(bf16[16,1,64]{2,0,1:T(8,128)(2,1)S(1)} %bitcast.44), channel_id=1, source_target_pairs={{0,1},{1,2},{2,3},{3,4},{4,5},{5,6},{6,7},{7,8},{8,9},{9,10},{10,1... | collective-permute-start | bytes 6152 | tf_op jit(solution)/shard_map/ppermute | solution.py:24
where the time goes:
time: 143 us; the launch traced here: 142 us
  blocking collectives  53.6 us (37%)
  local copies, waits for them, and re-layouts  25.1 us (18%)
  waiting for transfers between devices  24.1 us (17%)
  other arithmetic  22.5 us (16%)
  matrix products  9.64 us (7%)
  starting transfers between devices  6.4 us (4%)
    psum x5, blocking collectives, one_axis_at_a_time(): return functools.reduce(lax.psum, axes, x)  53.6 us
    all_to_all x1, waiting for transfers between devices, per_device(): lax.all_to_all(outgoing, GRP, split_axis=0, concat_axis=0, tiled=True)  19.1 us
    reshape x1, local copies, waits for them, and re-layouts, pooling(): shaped = tiles.reshape(count, planes, ROWS, COLS) * feather()  16.9 us
    reduce_sum x1, other arithmetic, pooling(): jnp.sum(shaped.reshape(count, planes, ROWS // 2, 2, COLS // 2, 2), axis=(...  16.5 us
    reduce_sum x1, local copies, waits for them, and re-layouts, pooling(): jnp.sum(shaped.reshape(count, planes, ROWS // 2, 2, COLS // 2, 2), axis=(...  5.12 us
    ppermute x1, waiting for transfers between devices, shifted(): lax.ppermute(value, axis, [(source, source + steps) for source in range(f...  5.01 us
    all_to_all x1, starting transfers between devices, per_device(): lax.all_to_all(outgoing, GRP, split_axis=0, concat_axis=0, tiled=True)  4.48 us
    dot_general x1, matrix products, per_device(): jnp.einsum('kx,tpx->tkp', basis, raw, preferred_element_type=jnp.float32)  4.13 us
  transfers between devices with their start and end apart: 2, of which 2 were waited for; matrix products, arithmetic and copies ran while one was open for 0% of the time, Pallas kernels for 0%

commit v1 on v0

v1 whole, which is shorter than its diff:
```python
import jax
import jax.numpy as jnp
from jax import lax
from jax.experimental import pallas as pl
from jax.experimental.pallas import tpu as pltpu
from jax.sharding import Mesh
from jax.sharding import PartitionSpec as P

ROWS = 2
COLS = 2048
OVL = 128
GRP = ("grp_0", "grp_1")
DEV = ("dev_0", "dev_1", "dev_2")
GRP_DEV = GRP + DEV
FIRST = ("dev_1", "dev_2")
SECOND = ("grp_0", "grp_1", "dev_0")
LANES = 128
WIDE = 256
HALF = LANES // 2


def terms_kernel(counts, raw, dark, basis, out):
    tiles, planes, pixels = raw.shape
    rank = basis.shape[0]
    ones = jnp.ones((rank, pixels), jnp.bfloat16)
    weights = jnp.concatenate([basis[...], ones], axis=0)
    contract = (((1,), (1,)), ((), ()))
    rows = lax.dot_general(
        raw[...].reshape(tiles * planes, pixels), weights, contract,
        preferred_element_type=jnp.float32,
    ).reshape(tiles, planes, 2 * rank)
    dark_rows = lax.dot_general(
        dark[...], weights, contract, preferred_element_type=jnp.float32
    )
    plane = lax.broadcasted_iota(jnp.int32, (planes, 2 * rank), 0)
    acc = jnp.zeros((planes, 2 * rank), jnp.float32)
    for t in range(tiles):
        acc = acc + jnp.where(plane < counts[t], rows[t] - dark_rows, 0.0)
    half = planes // 2
    pad = jnp.zeros((half, HALF - 2 * rank), jnp.float32)
    out[...] = jnp.concatenate([acc[:half], pad, acc[half:], pad], axis=1)


def pair_weights():
    row = lax.broadcasted_iota(jnp.int32, (WIDE, LANES), 0)
    col = lax.broadcasted_iota(jnp.int32, (WIDE, LANES), 1)
    hit = row // 2 == col
    up = (row.astype(jnp.float32) + 0.5) / OVL
    down = (WIDE - row.astype(jnp.float32) - 0.5) / OVL
    def of(scale):
        return jnp.where(hit, 0.25 * jnp.minimum(1.0, scale), 0.0).astype(jnp.bfloat16)
    return of(up), of(jnp.ones_like(up)), of(down)


def correct_kernel(counts, bands, parts, raw, dark, basis, corrected, cells, coef3, stage, sem):
    tiles, planes, pixels = raw.shape
    rank = basis.shape[0]
    half = planes // 2
    total = jnp.sum(parts[...], axis=0)
    terms = jnp.concatenate([total[:, :HALF], total[:, HALF:]], axis=0)
    coef = terms[:, :rank] / terms[:, rank : rank + 1]
    high = coef.astype(jnp.bfloat16)
    rest = coef - high.astype(jnp.float32)
    middle = rest.astype(jnp.bfloat16)
    low = (rest - middle.astype(jnp.float32)).astype(jnp.bfloat16)
    coef3[...] = jnp.concatenate([high, middle, low], axis=1)
    plane = lax.broadcasted_iota(jnp.int32, (planes, WIDE), 0)
    first, inner, last = pair_weights()
    blocks = COLS // WIDE
    copies = []
    for j in range(blocks):
        weight = first if j == 0 else last if j == blocks - 1 else inner
        acc = None
        for r in range(ROWS):
            x = slice(r * COLS + j * WIDE, r * COLS + (j + 1) * WIDE)
            base = basis[:, x]
            shade = jnp.dot(
                coef3[...], jnp.concatenate([base, base, base], axis=0),
                preferred_element_type=jnp.float32,
            )
            inverse = jnp.exp(-shade)
            dark_f = dark[:, x].astype(jnp.float32)
            for t in range(tiles):
                value = (raw[t, :, x].astype(jnp.float32) - dark_f) * inverse
                stage[t, :, x] = jnp.where(plane < counts[t], value, 0.0).astype(jnp.bfloat16)
            copy = pltpu.make_async_copy(
                stage.at[:, :, x], corrected.at[:, :, x], sem.at[j * ROWS + r]
            )
            copy.start()
            copies.append(copy)
            part = jnp.dot(
                stage[:, :, x].reshape(tiles * planes, WIDE), weight,
                preferred_element_type=jnp.float32,
            )
            acc = part if acc is None else acc + part
        pooled = acc.astype(jnp.bfloat16).reshape(tiles, planes, LANES)
        for t in range(tiles):
            cells[bands[t], :, j * LANES : (j + 1) * LANES] = pooled[t]
    for copy in copies:
        copy.wait()


def stitch_kernel(sources, arrived, spill, out):
    count, planes, width = arrived.shape
    step = (COLS - OVL) // 2
    lane = lax.broadcasted_iota(jnp.int32, (planes, LANES), 1)
    left = lane < HALF
    carry = jnp.where(left, pltpu.roll(spill[...].astype(jnp.float32), HALF, 1), 0.0)
    for j in range(0, count, 2):
        here = arrived[sources[j]].astype(jnp.float32)
        after = pltpu.roll(arrived[sources[j + 1]].astype(jnp.float32), HALF, 1)
        edge = after[:, :LANES]
        segment = jnp.concatenate(
            [
                here[:, :LANES] + carry,
                here[:, LANES : width - LANES],
                here[:, width - LANES :] + jnp.where(left, 0.0, edge),
                after[:, LANES:],
            ],
            axis=1,
        )
        out[:, j * step : (j + 2) * step] = segment.astype(jnp.bfloat16)
        carry = jnp.where(left, edge, 0.0)


SMEM = pl.BlockSpec(memory_space=pltpu.SMEM)
VMEM = pl.BlockSpec(memory_space=pltpu.VMEM)
ANY = pl.BlockSpec(memory_space=pl.ANY)


def summed_exchange(value, axes):
    copies = jnp.broadcast_to(value[None], (lax.axis_size(axes), *value.shape))
    return lax.all_to_all(copies, axes, split_axis=0, concat_axis=0, tiled=True)


def per_device(raw, dark, basis, counts, positions):
    tiles, planes, pixels = raw.shape
    groups = lax.axis_size(GRP)
    columns = lax.axis_size(DEV)
    band_size = columns * tiles
    width = COLS // 2
    terms = pl.pallas_call(
        terms_kernel,
        out_shape=jax.ShapeDtypeStruct((planes // 2, LANES), jnp.float32),
        in_specs=[SMEM, VMEM, VMEM, VMEM],
        out_specs=VMEM,
        name="terms",
    )(counts, raw, dark, basis)
    here_grp = lax.axis_index(GRP)
    here_dev = lax.axis_index(DEV)
    layout = positions.reshape(groups, columns, tiles)
    column_tiles = lax.dynamic_index_in_dim(layout, here_dev, 1, False)
    mine = lax.dynamic_index_in_dim(column_tiles, here_grp, 0, False)
    bands = mine // band_size
    arrives = column_tiles // band_size == here_grp
    slot_of = jnp.sum(jnp.where(arrives, column_tiles % tiles, 0), axis=1)
    slots = jnp.arange(tiles, dtype=jnp.int32)
    ids = jnp.arange(groups, dtype=jnp.int32)
    sources = jnp.sum(jnp.where(slot_of[None, :] == slots[:, None], ids[None, :], 0), axis=1)

    once = jnp.sum(summed_exchange(terms, FIRST), axis=0)
    parts = summed_exchange(once, SECOND)
    corrected, outgoing = pl.pallas_call(
        correct_kernel,
        out_shape=(
            jax.ShapeDtypeStruct(raw.shape, jnp.bfloat16),
            jax.ShapeDtypeStruct((groups, planes, width), jnp.bfloat16),
        ),
        in_specs=[SMEM, SMEM, VMEM, VMEM, VMEM, VMEM],
        out_specs=(ANY, VMEM),
        scratch_shapes=[
            pltpu.VMEM((planes, 3 * basis.shape[0]), jnp.bfloat16),
            pltpu.VMEM(raw.shape, jnp.bfloat16),
            pltpu.SemaphoreType.DMA((pixels // WIDE,)),
        ],
        name="correct",
    )(counts, bands, parts, raw, dark, basis)
    arrived = lax.all_to_all(outgoing, GRP, split_axis=0, concat_axis=0, tiled=True)
    tail = lax.dynamic_slice(
        arrived, (sources[tiles - 1], 0, width - LANES), (1, planes, LANES)
    )[0]
    spill = lax.ppermute(tail, DEV, [(d, d + 1) for d in range(columns - 1)])
    pooled = pl.pallas_call(
        stitch_kernel,
        out_shape=jax.ShapeDtypeStruct((planes, tiles * (COLS - OVL) // 2), jnp.bfloat16),
        in_specs=[SMEM, VMEM, VMEM],
        out_specs=VMEM,
        name="stitch",
    )(sources, arrived, spill)
    return corrected, pooled.reshape(1, planes, ROWS // 2, tiles * (COLS - OVL) // 2)


def solution(mesh):
    split = Mesh(mesh.devices.reshape(4, 4, 2, 8, 2), GRP_DEV)
    placed = (P(GRP_DEV, None, None), P(), P(), P(GRP_DEV), P())
    return jax.shard_map(
        per_device,
        mesh=split,
        in_specs=placed,
        out_specs=(P(GRP_DEV, None, None), P(GRP, None, None, DEV)),
        check_vma=False,
    )
```

time: 143 us -> 81.7 us (0.57)
  blocking collectives: 53.6 us -> 18 us
  local copies, waits for them, and re-layouts: 25.1 us -> 3.34 us
  other arithmetic: 22.5 us -> 0.81 us
  Pallas kernels: 0 us -> 10.6 us
  matrix products: 9.64 us -> 0 us
  starting transfers between devices: 6.4 us -> 15.7 us
  waiting for transfers between devices: 24.1 us -> 30.1 us
  between operations: 0.84 us -> 2.68 us
    psum x5 -> x0, blocking collectives: 53.6 us -> none  [one_axis_at_a_time(): return functools.reduce(lax.psum, axes, x)]
    reduce_sum x4 -> x3, other arithmetic: 18.6 us -> 0.26 us  [the longest x1 0.12 us: per_device(): slot_of = jnp.sum(jnp.where(arrives, column_tiles % tiles, 0), axis=1)]
    all_to_all x0 -> x1, blocking collectives: none -> 18 us  [summed_exchange(): return lax.all_to_all(copies, axes, split_axis=0, concat_axis=0, tiled=True)]
    reshape x2 -> x1, local copies, waits for them, and re-layouts: 17 us -> 0.12 us  [per_device(): layout = positions.reshape(groups, columns, tiles)]
    pallas_call x0 -> x3, Pallas kernels: none -> 10.6 us  [the longest x1 5.49 us: per_device(): pl.pallas_call(correct_kernel, out_shape=(jax.ShapeDtypeStruct(raw.shape,...]
    all_to_all x0 -> x1, starting transfers between devices: none -> 10.2 us  [summed_exchange(): return lax.all_to_all(copies, axes, split_axis=0, concat_axis=0, tiled=True)]
    dot_general x6 -> x0, matrix products: 9.64 us -> none  [the longest x1 4.13 us: per_device(): jnp.einsum('kx,tpx->tkp', basis, raw, preferred_element_type=jnp.float32)]
    all_to_all x0 -> x1, waiting for transfers between devices: none -> 9.56 us  [summed_exchange(): return lax.all_to_all(copies, axes, split_axis=0, concat_axis=0, tiled=True)]
  transfers between devices with their start and end apart: 2 -> 3, of which waited for: 2 -> 3; matrix products, arithmetic and copies ran while one was open for 0% -> 2% of each run, Pallas kernels for 0% -> 0%
where the time goes in v1:
time: 81.7 us; the launch traced here: 81.2 us
  waiting for transfers between devices  30.1 us (37%)
  blocking collectives  18 us (22%)
  starting transfers between devices  15.7 us (19%)
  Pallas kernels  10.6 us (13%)
  local copies, waits for them, and re-layouts  3.34 us (4%)
  between operations  2.68 us (3%)
    all_to_all x1, blocking collectives, summed_exchange(): return lax.all_to_all(copies, axes, split_axis=0, concat_axis=0, tiled=True)  18 us
    all_to_all x1, waiting for transfers between devices, per_device(): lax.all_to_all(outgoing, GRP, split_axis=0, concat_axis=0, tiled=True)  15.5 us
    all_to_all x1, starting transfers between devices, summed_exchange(): return lax.all_to_all(copies, axes, split_axis=0, concat_axis=0, tiled=True)  10.2 us
    all_to_all x1, waiting for transfers between devices, summed_exchange(): return lax.all_to_all(copies, axes, split_axis=0, concat_axis=0, tiled=True)  9.56 us
    pallas_call x1, Pallas kernels, per_device(): pl.pallas_call(correct_kernel, out_shape=(jax.ShapeDtypeStruct(raw.shape,...  5.49 us
    ppermute x1, waiting for transfers between devices, per_device(): spill = lax.ppermute(tail, DEV, [(d, d + 1) for d in range(columns - 1)])  5.11 us
    all_to_all x1, starting transfers between devices, per_device(): lax.all_to_all(outgoing, GRP, split_axis=0, concat_axis=0, tiled=True)  3.58 us
    pallas_call x1, Pallas kernels, per_device(): pl.pallas_call(terms_kernel, out_shape=jax.ShapeDtypeStruct((planes // 2,...  3.12 us
  transfers between devices with their start and end apart: 3, of which 3 were waited for; matrix products, arithmetic and copies ran while one was open for 2% of the time, Pallas kernels for 0%

profile of v1, /device:TPU:8, one launch (start us, length us, event | category | flops | bytes accessed | tf_op | source)
XLA Modules:
  0.0 81.2 jit_solution(7280717485179449245)
XLA Ops:
  0.6 0.0 copy-start.2
  0.6 3.1 %terms.1 = f32[8,128]{1,0:T(8,128)} custom-call(s32[16]{0:T(128)} %counts.3, bf16[16,16,4096]{2,1,0:T(8,128)(2,1)} %raw.3, bf16[16,4096]{1,0:T(8,128)(2,1)} %dark.3, bf16[8,4096]{1,0:T(8,128)(2,1)} %basis.3), custom_call_target="tpu_custom_call" | custom-call | tf_op jit(solution)/shard_map/terms/pallas_call | solution.py:142
  3.8 0.7 broadcast_in_dim.16
  4.4 18.0 %all_to_all.15 = f32[16,8,128]{2,1,0:T(8,128)S(1)} all-to-all(f32[16,8,128]{2,1,0:T(8,128)S(1)} %broadcast_in_dim.16), channel_id=1, replica_groups=mesh['grp_0'=4,'grp_1'=4,'dev_0'=2,'dev_1'=8,'dev_2'=2] {'dev_1','dev_2'}, dimensions={0} | all-to-all | bytes 131072 | tf_op jit(solution)/shard_map/all_to_all | solution.py:133
  22.5 0.7 broadcast_in_dim.17
  23.1 10.2 %all-to-all-start.1 = ((f32[32,8,128]{2,1,0:T(8,128)}), f32[32,8,128]{2,1,0:T(8,128)S(1)}, u32[]{:S(2)}, u32[]{:S(2)}) async-start(f32[32,8,128]{2,1,0:T(8,128)} %broadcast_in_dim.17), calls=%async_computation.1 | async-start | bytes 262144 | tf_op jit(solution)/shard_map/all_to_all | solution.py:133
  33.3 0.0 copy-done.2
  33.3 0.1 reshape.15
  33.5 0.6 and_select_fusion.bands
  34.0 9.6 %all-to-all-done.1.parts = f32[32,8,128]{2,1,0:T(8,128)S(1)} async-done(((f32[32,8,128]{2,1,0:T(8,128)}), f32[32,8,128]{2,1,0:T(8,128)S(1)}, u32[]{:S(2)}, u32[]{:S(2)}) %all-to-all-start.1) | async-done | bytes 131104 | tf_op jit(solution)/shard_map/all_to_all | solution.py:133
  43.6 0.0 copy-start.1
  43.6 0.7 copy-done.1
  44.2 5.5 %correct.1 = (bf16[16,16,4096]{2,1,0:T(8,128)(2,1)}, bf16[16,16,1024]{2,1,0:T(8,128)(2,1)}) custom-call(s32[16]{0:T(128)} %counts.3, s32[16]{0:T(128)} %and_select_fusion.bands, f32[32,8,128]{2,1,0:T(8,128)} %copy-done.1, bf16[16,16,4096]{2,1,0:T(8,128)(2,1)} %raw.3, bf16[16,4096]{1,0:T(8,128)(2,1)} %dark.3, bf16[8,4096]{1,0:T(8,128)(2,1)} %basis.3), custom_call_target="tpu_custom_call" | custom-call | tf_op jit(solution)/shard_map/correct/pallas_call | solution.py:163
  49.7 3.6 %all-to-all-start.2 = ((bf16[16,16,1024]{2,1,0:T(8,128)(2,1)}), bf16[16,16,1024]{2,1,0:T(8,128)(2,1)S(1)}, u32[]{:S(2)}, u32[]{:S(2)}) async-start(bf16[16,16,1024]{2,1,0:T(8,128)(2,1)} %get-tuple-element.5), calls=%async_computation.2 | async-start | bytes 1048576 | tf_op jit(solution)/shard_map/all_to_all | solution.py:178
  53.4 0.1 fusion.3
  53.5 0.1 select_reduce_fusion.sources
  53.6 0.0 copy-start.4
  53.6 0.6 slice.3
  56.1 15.5 %all-to-all-done.2.arrived = bf16[16,16,1024]{2,1,0:T(8,128)(2,1)S(1)} async-done(((bf16[16,16,1024]{2,1,0:T(8,128)(2,1)}), bf16[16,16,1024]{2,1,0:T(8,128)(2,1)S(1)}, u32[]{:S(2)}, u32[]{:S(2)}) %all-to-all-start.2) | async-done | bytes 524320 | tf_op jit(solution)/shard_map/all_to_all | solution.py:178
  71.6 0.0 copy-start
  71.6 1.9 %collective-permute-start = (bf16[16,128]{1,0:T(8,128)(2,1)S(1)}, bf16[16,128]{1,0:T(8,128)(2,1)S(1)}, u32[]{:S(2)}, u32[]{:S(2)}) collective-permute-start(bf16[16,128]{1,0:T(8,128)(2,1)S(1)} %dynamic-slice_bitcast_fusion), channel_id=1, source_target_pairs={{0,1},{1,2},{2,3},{3,4},{4,5},{5,6},{6,7},{7,8},{8,9},{9,10},{10,1... | collective-permute-start | bytes 12296 | tf_op jit(solution)/shard_map/ppermute | solution.py:182
  73.5 5.1 %collective-permute-done.spill = bf16[16,128]{1,0:T(8,128)(2,1)S(1)} collective-permute-done((bf16[16,128]{1,0:T(8,128)(2,1)S(1)}, bf16[16,128]{1,0:T(8,128)(2,1)S(1)}, u32[]{:S(2)}, u32[]{:S(2)}) %collective-permute-start) | collective-permute-done | bytes 4128 | tf_op jit(solution)/shard_map/ppermute | solution.py:182
  78.6 0.0 copy-done.4
  78.6 0.0 copy-done
  78.7 0.0 copy-start.3
  78.7 0.6 copy-done.3
  79.2 2.0 %stitch.1 = bf16[16,15360]{1,0:T(8,128)(2,1)} custom-call(s32[16]{0:T(128)} %copy-done.4, bf16[16,16,1024]{2,1,0:T(8,128)(2,1)} %copy-done, bf16[16,128]{1,0:T(8,128)(2,1)} %copy-done.3), custom_call_target="tpu_custom_call" | custom-call | tf_op jit(solution)/shard_map/stitch/pallas_call | solution.py:183
  (3 shorter events, 0.0 us)
Async XLA Ops:
  0.6 32.7 %copy-start.2 = (s32[8192]{0:T(1024)S(1)}, s32[8192]{0:T(1024)}, u32[]{:S(2)}) copy-start(s32[8192]{0:T(1024)} %param.9) | copy-start | bytes 98308
  23.1 20.5 %all-to-all-start.1 = ((f32[32,8,128]{2,1,0:T(8,128)}), f32[32,8,128]{2,1,0:T(8,128)S(1)}, u32[]{:S(2)}, u32[]{:S(2)}) async-start(f32[32,8,128]{2,1,0:T(8,128)} %broadcast_in_dim.17), calls=%async_computation.1 | async-start | bytes 262144 | tf_op jit(solution)/shard_map/all_to_all | solution.py:133
  43.6 0.7 copy-start.1
  49.7 21.9 %all-to-all-start.2 = ((bf16[16,16,1024]{2,1,0:T(8,128)(2,1)}), bf16[16,16,1024]{2,1,0:T(8,128)(2,1)S(1)}, u32[]{:S(2)}, u32[]{:S(2)}) async-start(bf16[16,16,1024]{2,1,0:T(8,128)(2,1)} %get-tuple-element.5), calls=%async_computation.2 | async-start | bytes 1048576 | tf_op jit(solution)/shard_map/all_to_all | solution.py:178
  53.6 25.0 %copy-start.4 = (s32[16]{0:T(128)}, s32[16]{0:T(128)S(1)}, u32[]{:S(2)}) copy-start(s32[16]{0:T(128)S(1)} %select_reduce_fusion.sources) | copy-start | bytes 196
  71.6 7.0 %copy-start = (bf16[16,16,1024]{2,1,0:T(8,128)(2,1)}, bf16[16,16,1024]{2,1,0:T(8,128)(2,1)S(1)}, u32[]{:S(2)}) copy-start(bf16[16,16,1024]{2,1,0:T(8,128)(2,1)S(1)} %all-to-all-done.2.arrived) | copy-start | bytes 1572868
  71.6 7.0 %collective-permute-start = (bf16[16,128]{1,0:T(8,128)(2,1)S(1)}, bf16[16,128]{1,0:T(8,128)(2,1)S(1)}, u32[]{:S(2)}, u32[]{:S(2)}) collective-permute-start(bf16[16,128]{1,0:T(8,128)(2,1)S(1)} %dynamic-slice_bitcast_fusion), channel_id=1, source_target_pairs={{0,1},{1,2},{2,3},{3,4},{4,5},{5,6},{6,7},{7,8},{8,9},{9,10},{10,1... | collective-permute-start | bytes 12296 | tf_op jit(solution)/shard_map/ppermute | solution.py:182
  78.7 0.6 copy-start.3

commit v2 on v1

v2 whole, which is shorter than its diff:
```python
import jax
import jax.numpy as jnp
from jax import lax
from jax.experimental import pallas as pl
from jax.experimental.pallas import tpu as pltpu
from jax.sharding import Mesh
from jax.sharding import PartitionSpec as P

ROWS = 2
COLS = 2048
OVL = 128
GRP = ("grp_0", "grp_1")
DEV = ("dev_0", "dev_1", "dev_2")
GRP_DEV = GRP + DEV
FIRST = ("dev_1", "dev_2")
SECOND = ("grp_0", "grp_1", "dev_0")
LANES = 128
WIDE = 256
HALF = LANES // 2
SUBLANES = 8
PARTS = 16
CHUNKS = 4


def packed(rows):
    planes = rows.shape[0]
    lane = lax.broadcasted_iota(jnp.int32, (planes, LANES), 1)
    plane = lax.broadcasted_iota(jnp.int32, (planes, LANES), 0)
    wide = jnp.where(lane < PARTS, rows, 0.0)
    for shift in (PARTS, 2 * PARTS, 4 * PARTS):
        wide = wide + pltpu.roll(wide, shift, 1)
    chosen = jnp.where(lane // PARTS == plane % SUBLANES, wide, 0.0)
    return jnp.sum(chosen.reshape(planes // SUBLANES, SUBLANES, LANES), axis=1)


def unpacked(rows):
    count = rows.shape[0]
    planes = count * SUBLANES
    lane = lax.broadcasted_iota(jnp.int32, (planes, LANES), 1)
    plane = lax.broadcasted_iota(jnp.int32, (planes, LANES), 0)
    spread = jnp.broadcast_to(rows[:, None, :], (count, SUBLANES, LANES)).reshape(planes, LANES)
    wide = jnp.where(lane // PARTS == plane % SUBLANES, spread, 0.0)
    for shift in (PARTS, 2 * PARTS, 4 * PARTS):
        wide = wide + pltpu.roll(wide, shift, 1)
    return wide


def terms_kernel(
    counts_h, raw_h, dark_h, basis_h, out, raw, dark, basis, edges, counts, sem
):
    tiles, planes, pixels = raw.shape
    rank = basis.shape[0]
    chunk = tiles // CHUNKS
    small = [
        pltpu.make_async_copy(basis_h, basis, sem.at[CHUNKS]),
        pltpu.make_async_copy(dark_h, dark, sem.at[CHUNKS + 1]),
        pltpu.make_async_copy(counts_h, counts, sem.at[CHUNKS + 2]),
    ]
    large = []
    for c in range(CHUNKS):
        t = slice(c * chunk, (c + 1) * chunk)
        large.append(pltpu.make_async_copy(raw_h.at[t], raw.at[t], sem.at[c]))
    for copy in small + large:
        copy.start()
    for copy in small:
        copy.wait()
    weights = jnp.concatenate([basis[...], jnp.ones((rank, pixels), jnp.bfloat16)], axis=0)
    contract = (((1,), (1,)), ((), ()))
    dark_rows = lax.dot_general(
        dark[...], weights, contract, preferred_element_type=jnp.float32
    )
    plane = lax.broadcasted_iota(jnp.int32, (planes, 2 * rank), 0)
    wide_plane = lax.broadcasted_iota(jnp.int32, (planes, OVL), 0)
    acc = jnp.zeros((planes, 2 * rank), jnp.float32)
    ends = [slice((r + 1) * COLS - OVL, (r + 1) * COLS) for r in range(ROWS)]
    dark_ends = [dark[:, x].astype(jnp.float32) for x in ends]
    for c in range(CHUNKS):
        large[c].wait()
        t0 = c * chunk
        rows = lax.dot_general(
            raw[t0 : t0 + chunk].reshape(chunk * planes, pixels), weights, contract,
            preferred_element_type=jnp.float32,
        ).reshape(chunk, planes, 2 * rank)
        for i in range(chunk):
            t = t0 + i
            acc = acc + jnp.where(plane < counts[t], rows[i] - dark_rows, 0.0)
            for r in range(ROWS):
                value = raw[t, :, ends[r]].astype(jnp.float32)
                kept = jnp.where(wide_plane < counts[t], value, dark_ends[r])
                edges[t, :, r * OVL : (r + 1) * OVL] = kept.astype(jnp.bfloat16)
    pad = jnp.zeros((planes, LANES - 2 * rank), jnp.float32)
    rows = packed(jnp.concatenate([acc, pad], axis=1))
    out[...] = jnp.broadcast_to(rows[None], out.shape)


def pair_weights():
    row = lax.broadcasted_iota(jnp.int32, (WIDE, LANES), 0)
    col = lax.broadcasted_iota(jnp.int32, (WIDE, LANES), 1)
    hit = row // 2 == col
    up = (row.astype(jnp.float32) + 0.5) / OVL
    down = (WIDE - row.astype(jnp.float32) - 0.5) / OVL
    def of(scale):
        return jnp.where(hit, 0.25 * jnp.minimum(1.0, scale), 0.0).astype(jnp.bfloat16)
    return of(up), of(jnp.ones_like(up)), of(down)


def tail_weights():
    row = lax.broadcasted_iota(jnp.int32, (ROWS * OVL, LANES), 0) % OVL
    col = lax.broadcasted_iota(jnp.int32, (ROWS * OVL, LANES), 1) % HALF
    scale = jnp.minimum(1.0, (OVL - row.astype(jnp.float32) - 0.5) / OVL)
    return jnp.where(row // 2 == col, 0.25 * scale, 0.0).astype(jnp.bfloat16)


def correct_kernel(
    counts_h, positions_h, parts, raw, dark, basis, edges, corrected_h, cells_h,
    corrected, cells, inverse, counts, positions, sem,
):
    tiles, planes, pixels = raw.shape
    rank = basis.shape[0]
    half = planes // 2
    copies = [
        pltpu.make_async_copy(counts_h, counts, sem.at[0]),
        pltpu.make_async_copy(positions_h, positions, sem.at[1]),
    ]
    for copy in copies:
        copy.start()
    columns = lax.axis_size(DEV)
    own = (lax.axis_index(GRP) * columns + lax.axis_index(DEV)) * tiles
    before = jnp.maximum(own - tiles, 0)
    terms = unpacked(jnp.sum(parts[...], axis=0))
    coef = (terms / pltpu.roll(terms, LANES - rank, 1))[:, :rank]
    high = coef.astype(jnp.bfloat16)
    rest = coef - high.astype(jnp.float32)
    middle = rest.astype(jnp.bfloat16)
    low = (rest - middle.astype(jnp.float32)).astype(jnp.bfloat16)
    coef3 = jnp.concatenate([high, middle, low], axis=1)
    base = basis[...]
    shade = jnp.dot(
        coef3, jnp.concatenate([base, base, base], axis=0), preferred_element_type=jnp.float32
    )
    inverse[...] = jnp.exp(-shade)
    leaving = []

    def leave(source, target):
        copy = pltpu.make_async_copy(source, target, sem.at[2 + len(leaving)])
        copy.start()
        leaving.append(copy)

    ends = [slice((r + 1) * COLS - OVL, (r + 1) * COLS) for r in range(ROWS)]
    value = jnp.concatenate(
        [
            ((edges[:, :, r * OVL : (r + 1) * OVL].astype(jnp.float32)
              - dark[:, x].astype(jnp.float32)[None]) * inverse[:, x][None]).astype(jnp.bfloat16)
            for r, x in enumerate(ends)
        ],
        axis=2,
    )
    tails = jnp.dot(
        value.reshape(tiles * planes, ROWS * OVL), tail_weights(),
        preferred_element_type=jnp.float32,
    ).reshape(tiles, planes, LANES)
    left = lax.broadcasted_iota(jnp.int32, (half, LANES), 1) < HALF
    for copy in copies:
        copy.wait()
    for t in range(tiles):
        band = positions[before + t] // (columns * tiles)
        joined = jnp.where(left, tails[t, :half], tails[t, half:])
        cells[band, COLS // WIDE * planes :, :] = joined.astype(jnp.bfloat16)
    plane = lax.broadcasted_iota(jnp.int32, (planes, WIDE), 0)
    first, inner, last = pair_weights()
    blocks = COLS // WIDE
    for j in range(blocks):
        weight = first if j == 0 else last if j == blocks - 1 else inner
        acc = None
        for r in range(ROWS):
            x = slice(r * COLS + j * WIDE, r * COLS + (j + 1) * WIDE)
            scale = inverse[:, x]
            dark_f = dark[:, x].astype(jnp.float32)
            for t in range(tiles):
                value = (raw[t, :, x].astype(jnp.float32) - dark_f) * scale
                corrected[t, :, x] = jnp.where(plane < counts[t], value, 0.0).astype(jnp.bfloat16)
            leave(corrected.at[:, :, x], corrected_h.at[:, :, x])
            part = jnp.dot(
                corrected[:, :, x].reshape(tiles * planes, WIDE), weight,
                preferred_element_type=jnp.float32,
            )
            acc = part if acc is None else acc + part
        pooled = acc.astype(jnp.bfloat16).reshape(tiles, planes, LANES)
        for t in range(tiles):
            band = positions[own + t] // (columns * tiles)
            cells[band, j * planes : (j + 1) * planes, :] = pooled[t]
        x = slice(j * planes, (j + 1) * planes + (half if j == blocks - 1 else 0))
        leave(cells.at[:, x, :], cells_h.at[:, x, :])
    for copy in leaving:
        copy.wait()


def stitch_kernel(sources, arrived, out_h, out, sem):
    planes = out.shape[0]
    count = arrived.shape[0]
    half = planes // 2
    blocks = COLS // 2 // LANES
    step = (COLS - OVL) // 2
    lane = lax.broadcasted_iota(jnp.int32, (planes, LANES), 1)
    left = lane < HALF

    def tile(source):
        return jnp.concatenate(
            [arrived[source, j * planes : (j + 1) * planes, :] for j in range(blocks)], axis=1
        ).astype(jnp.float32)

    spill = arrived[sources[count], blocks * planes :, :].astype(jnp.float32)
    spill = jnp.concatenate([spill, pltpu.roll(spill, HALF, 1)], axis=0)
    carry = jnp.where(left & (lax.axis_index(DEV) > 0), spill, 0.0)
    copies = []
    for j in range(0, count, 2):
        here = tile(sources[j])
        after = pltpu.roll(tile(sources[j + 1]), HALF, 1)
        edge = after[:, :LANES]
        width = here.shape[1]
        segment = jnp.concatenate(
            [
                here[:, :LANES] + carry,
                here[:, LANES : width - LANES],
                here[:, width - LANES :] + jnp.where(left, 0.0, edge),
                after[:, LANES:],
            ],
            axis=1,
        )
        x = slice(j * step, (j + 2) * step)
        out[:, x] = segment.astype(jnp.bfloat16)
        copy = pltpu.make_async_copy(out.at[:, x], out_h.at[:, x], sem.at[j // 2])
        copy.start()
        copies.append(copy)
        carry = jnp.where(left, edge, 0.0)
    for copy in copies:
        copy.wait()


SMEM = pl.BlockSpec(memory_space=pltpu.SMEM)
VMEM = pl.BlockSpec(memory_space=pltpu.VMEM)
HBM = pl.BlockSpec(memory_space=pltpu.HBM)
LIMIT = pltpu.CompilerParams(vmem_limit_bytes=16 << 20)


def in_vmem(value):
    return pltpu.with_memory_space_constraint(value, pltpu.VMEM)


def in_hbm(value):
    return pltpu.with_memory_space_constraint(value, pltpu.HBM)


def exchanged(copies, axes):
    return lax.all_to_all(copies, axes, split_axis=0, concat_axis=0, tiled=True)


def sources_of(positions, column, groups, columns, tiles):
    layout = positions.reshape(groups, columns, tiles)
    column_tiles = lax.dynamic_index_in_dim(layout, column, 1, False)
    arrives = column_tiles // (columns * tiles) == lax.axis_index(GRP)
    slot_of = jnp.sum(jnp.where(arrives, column_tiles % tiles, 0), axis=1)
    slots = jnp.arange(tiles, dtype=jnp.int32)
    ids = jnp.arange(groups, dtype=jnp.int32)
    return jnp.sum(jnp.where(slot_of[None, :] == slots[:, None], ids[None, :], 0), axis=1)


def per_device(raw, dark, basis, counts, positions):
    tiles, planes, pixels = raw.shape
    groups = lax.axis_size(GRP)
    columns = lax.axis_size(DEV)
    width = COLS // 2
    span = tiles * (COLS - OVL) // 2
    height = width // LANES * planes + planes // 2
    first, second = lax.axis_size(FIRST), lax.axis_size(SECOND)
    terms, raw_v, dark_v, basis_v, edges = pl.pallas_call(
        terms_kernel,
        out_shape=(
            pltpu.VMEM((first, planes // SUBLANES, LANES), jnp.float32),
            pltpu.VMEM(raw.shape, jnp.bfloat16),
            pltpu.VMEM(dark.shape, jnp.bfloat16),
            pltpu.VMEM(basis.shape, jnp.bfloat16),
            jax.ShapeDtypeStruct((tiles, planes, ROWS * OVL), jnp.bfloat16),
        ),
        in_specs=[HBM, HBM, HBM, HBM],
        out_specs=(VMEM, VMEM, VMEM, VMEM, VMEM),
        scratch_shapes=[
            pltpu.SMEM((tiles,), jnp.int32),
            pltpu.SemaphoreType.DMA((CHUNKS + 3,)),
        ],
        compiler_params=LIMIT,
        name="terms",
    )(in_hbm(counts), in_hbm(raw), in_hbm(dark), in_hbm(basis))
    once = jnp.sum(exchanged(terms, FIRST), axis=0)
    edges, positions_late, once = lax.optimization_barrier((edges, positions, once))
    parts = exchanged(jnp.broadcast_to(once[None], (second, *once.shape)), SECOND)
    edges = lax.ppermute(edges, DEV, [(d, d + 1) for d in range(columns - 1)])
    here_dev = lax.axis_index(DEV)
    own_sources = sources_of(positions_late, here_dev, groups, columns, tiles)
    left_dev = jnp.maximum(here_dev - 1, 0)
    left_sources = sources_of(positions_late, left_dev, groups, columns, tiles)
    sources = jnp.concatenate([own_sources, left_sources[tiles - 1 :]])
    corrected, outgoing = pl.pallas_call(
        correct_kernel,
        out_shape=(
            jax.ShapeDtypeStruct(raw.shape, jnp.bfloat16),
            jax.ShapeDtypeStruct((groups, height, LANES), jnp.bfloat16),
        ),
        in_specs=[HBM, HBM, VMEM, VMEM, VMEM, VMEM, VMEM],
        out_specs=(HBM, HBM),
        scratch_shapes=[
            pltpu.VMEM(raw.shape, jnp.bfloat16),
            pltpu.VMEM((groups, height, LANES), jnp.bfloat16),
            pltpu.VMEM(dark.shape, jnp.float32),
            pltpu.SMEM((tiles,), jnp.int32),
            pltpu.SMEM(positions.shape, jnp.int32),
            pltpu.SemaphoreType.DMA((2 + pixels // WIDE + width // LANES,)),
        ],
        compiler_params=LIMIT,
        name="correct",
    )(
        in_hbm(counts), in_hbm(positions), in_vmem(parts), in_vmem(raw_v), in_vmem(dark_v),
        in_vmem(basis_v), in_vmem(edges),
    )
    arrived = exchanged(outgoing, GRP)
    pooled = pl.pallas_call(
        stitch_kernel,
        out_shape=jax.ShapeDtypeStruct((planes, span), jnp.bfloat16),
        in_specs=[SMEM, VMEM],
        out_specs=HBM,
        scratch_shapes=[
            pltpu.VMEM((planes, span), jnp.bfloat16),
            pltpu.SemaphoreType.DMA((tiles // 2,)),
        ],
        compiler_params=LIMIT,
        name="stitch",
    )(sources, in_vmem(arrived))
    return corrected, pooled.reshape(1, planes, ROWS // 2, span)


def solution(mesh):
    split = Mesh(mesh.devices.reshape(4, 4, 2, 8, 2), GRP_DEV)
    placed = (P(GRP_DEV, None, None), P(), P(), P(GRP_DEV), P())
    return jax.shard_map(
        per_device,
        mesh=split,
        in_specs=placed,
        out_specs=(P(GRP_DEV, None, None), P(GRP, None, None, DEV)),
        check_vma=False,
    )
```

time: 81.7 us -> 70.9 us (0.87)
  the two profiles are of different devices: /device:TPU:8 before, /device:TPU:1 now
where the time goes in v2:
time: 70.9 us; the launch traced here: 70.5 us
  blocking collectives  37.2 us (52%)
  waiting for transfers between devices  16 us (23%)
  Pallas kernels  8.61 us (12%)
  starting transfers between devices  6.04 us (9%)
  other arithmetic  1.11 us (2%)
  local copies, waits for them, and re-layouts  0.76 us (1%)
  between operations  0.72 us (1%)
    all_to_all x2, blocking collectives, exchanged(): return lax.all_to_all(copies, axes, split_axis=0, concat_axis=0, tiled=True)  37.2 us
    all_to_all x1, waiting for transfers between devices, exchanged(): return lax.all_to_all(copies, axes, split_axis=0, concat_axis=0, tiled=True)  16 us
    pallas_call x1, Pallas kernels, per_device(): pl.pallas_call(correct_kernel, out_shape=(jax.ShapeDtypeStruct(raw.shape,...  4.16 us
    all_to_all x1, starting transfers between devices, exchanged(): return lax.all_to_all(copies, axes, split_axis=0, concat_axis=0, tiled=True)  3.59 us
    pallas_call x1, Pallas kernels, per_device(): pl.pallas_call(terms_kernel, out_shape=(pltpu.VMEM((first, planes // SUBL...  2.99 us
    ppermute x1, starting transfers between devices, per_device(): edges = lax.ppermute(edges, DEV, [(d, d + 1) for d in range(columns - 1)])  2.45 us
    pallas_call x1, Pallas kernels, per_device(): pl.pallas_call(stitch_kernel, out_shape=jax.ShapeDtypeStruct((planes, spa...  1.47 us
  transfers between devices with their start and end apart: 2, of which 1 were waited for; matrix products, arithmetic and copies ran while one was open for 3% of the time, Pallas kernels for 0%

profile of v2, /device:TPU:1, one launch (start us, length us, event | category | flops | bytes accessed | tf_op | source)
XLA Modules:
  0.0 70.5 jit_solution(12772925777977596428)
XLA Ops:
  0.6 3.0 %terms.1 = (f32[16,2,128]{2,1,0:T(2,128)S(1)}, bf16[16,16,4096]{2,1,0:T(8,128)(2,1)S(1)}, bf16[16,4096]{1,0:T(8,128)(2,1)S(1)}, bf16[8,4096]{1,0:T(8,128)(2,1)S(1)}, bf16[16,16,256]{2,1,0:T(8,128)(2,1)S(1)}) custom-call(s32[16]{0:T(128)} %counts_h.3, bf16[16,16,4096]{2,1,0:T(8,128)(2,1)} %raw_h.1, bf16[16,4096]{1,0:T(8,128)(2,1)} %dark_h.1, ...), custom_call_target="tpu_custom_call" | custom-call | tf_op jit(solution)/shard_map/terms/pallas_call | solution.py:276
  3.6 0.0 copy-start
  3.6 18.9 %all_to_all.15 = f32[16,2,128]{2,1,0:T(2,128)S(1)} all-to-all(f32[16,2,128]{2,1,0:T(2,128)S(1)} %get-tuple-element.13), channel_id=1, replica_groups=mesh['grp_0'=4,'grp_1'=4,'dev_0'=2,'dev_1'=8,'dev_2'=2] {'dev_1','dev_2'}, dimensions={0} | all-to-all | bytes 32768 | tf_op jit(solution)/shard_map/all_to_all | solution.py:255
  22.6 2.5 %collective-permute-start = (bf16[16,16,256]{2,1,0:T(8,128)(2,1)S(1)}, bf16[16,16,256]{2,1,0:T(8,128)(2,1)S(1)}, u32[]{:S(2)}, u32[]{:S(2)}) collective-permute-start(bf16[16,16,256]{2,1,0:T(8,128)(2,1)S(1)} %get-tuple-element.18), channel_id=1, source_target_pairs={{0,1},{1,2},{2,3},{3,4},{4,5},{5,6},{6,7},{7,8},{8,9},{9,10},{10,1... | collective-permute-start | bytes 393224 | tf_op jit(solution)/shard_map/ppermute | solution.py:297
  25.1 18.2 %all_to_all.16.parts = f32[32,2,128]{2,1,0:T(2,128)S(1)} all-to-all(f32[32,2,128]{2,1,0:T(2,128)S(1)} %broadcast_in_dim.31), channel_id=1, replica_groups=mesh['grp_0'=4,'grp_1'=4,'dev_0'=2,'dev_1'=8,'dev_2'=2] {'grp_0','grp_1'..., dimensions={0} | all-to-all | bytes 65536 | tf_op jit(solution)/shard_map/all_to_all | solution.py:255
  43.3 0.0 collective-permute-done.edges
  43.3 4.2 %correct.1 = (bf16[16,16,4096]{2,1,0:T(8,128)(2,1)}, bf16[16,136,128]{2,1,0:T(8,128)(2,1)}) custom-call(s32[16]{0:T(128)} %counts_h.3, s32[8192]{0:T(1024)} %positions_h.1, f32[32,2,128]{2,1,0:T(2,128)S(1)} %all_to_all.16.parts, bf16[16,16,4096]{2,1,0:T(8,128)(2,1)S(1)} %get-tuple-element.15.raw, bf16[16,4096]{1,0:T(8,128)(2,1)S(1)} %get-tuple-element.16.dark, ...), custom_call_target="tpu_custom_call" | custom-call | tf_op jit(solution)/shard_map/correct/pallas_call | solution.py:303
  47.5 3.6 %all-to-all-start.2 = ((bf16[16,136,128]{2,1,0:T(8,128)(2,1)}), bf16[16,136,128]{2,1,0:T(8,128)(2,1)S(1)}, u32[]{:S(2)}, u32[]{:S(2)}) async-start(bf16[16,136,128]{2,1,0:T(8,128)(2,1)} %get-tuple-element.21), calls=%async_computation.2 | async-start | bytes 1114112 | tf_op jit(solution)/shard_map/all_to_all | solution.py:255
  51.1 0.0 copy-done
  51.1 0.1 reshape.14
  51.3 0.1 fusion.3
  51.4 0.1 select_reduce_fusion
  51.5 0.6 slice.3
  52.1 0.1 select_reduce_fusion.1
  52.2 0.7 %pad_add_fusion.sources = s32[17]{0:T(128)S(1)} fusion(s32[1]{0:T(128)} %slice.3, s32[16]{0:T(128)S(1)} %select_reduce_fusion.1), kind=kLoop, calls=%fused_computation.30 | loop fusion | flops 17 | bytes 136 | tf_op jit(solution)/shard_map/concatenate | solution.py:302
  53.0 16.0 %all-to-all-done.2.arrived = bf16[16,136,128]{2,1,0:T(8,128)(2,1)S(1)} async-done(((bf16[16,136,128]{2,1,0:T(8,128)(2,1)}), bf16[16,136,128]{2,1,0:T(8,128)(2,1)S(1)}, u32[]{:S(2)}, u32[]{:S(2)}) %all-to-all-start.2) | async-done | bytes 557088 | tf_op jit(solution)/shard_map/all_to_all | solution.py:255
  69.0 1.5 %stitch.1 = bf16[16,15360]{1,0:T(8,128)(2,1)} custom-call(s32[17]{0:T(128)S(1)} %pad_add_fusion.sources, bf16[16,136,128]{2,1,0:T(8,128)(2,1)S(1)} %all-to-all-done.2.arrived), custom_call_target="tpu_custom_call" | custom-call | tf_op jit(solution)/shard_map/stitch/pallas_call | solution.py:326
  (3 shorter events, 0.1 us)
Async XLA Ops:
  3.6 47.5 %copy-start = (s32[8192]{0:T(1024)S(1)}, s32[8192]{0:T(1024)}, u32[]{:S(2)}) copy-start(s32[8192]{0:T(1024)} %positions_h.1) | copy-start | bytes 98308
  22.6 20.7 %collective-permute-start = (bf16[16,16,256]{2,1,0:T(8,128)(2,1)S(1)}, bf16[16,16,256]{2,1,0:T(8,128)(2,1)S(1)}, u32[]{:S(2)}, u32[]{:S(2)}) collective-permute-start(bf16[16,16,256]{2,1,0:T(8,128)(2,1)S(1)} %get-tuple-element.18), channel_id=1, source_target_pairs={{0,1},{1,2},{2,3},{3,4},{4,5},{5,6},{6,7},{7,8},{8,9},{9,10},{10,1... | collective-permute-start | bytes 393224 | tf_op jit(solution)/shard_map/ppermute | solution.py:297
  47.5 21.5 %all-to-all-start.2 = ((bf16[16,136,128]{2,1,0:T(8,128)(2,1)}), bf16[16,136,128]{2,1,0:T(8,128)(2,1)S(1)}, u32[]{:S(2)}, u32[]{:S(2)}) async-start(bf16[16,136,128]{2,1,0:T(8,128)(2,1)} %get-tuple-element.21), calls=%async_computation.2 | async-start | bytes 1114112 | tf_op jit(solution)/shard_map/all_to_all | solution.py:255

commit v3 on v2

--- a/solution.py
+++ b/solution.py
@@ -20,6 +20,7 @@
 SUBLANES = 8
 PARTS = 16
 CHUNKS = 4
+EARLY = 3
 
 
 def packed(rows):
@@ -46,15 +47,15 @@
 
 
 def terms_kernel(
-    counts_h, raw_h, dark_h, basis_h, out, raw, dark, basis, edges, counts, sem
+    counts_h, raw_h, dark_h, basis_h, out, raw, dark, basis, edges, limits, counts, sem
 ):
     tiles, planes, pixels = raw.shape
     rank = basis.shape[0]
     chunk = tiles // CHUNKS
     small = [
-        pltpu.make_async_copy(basis_h, basis, sem.at[CHUNKS]),
-        pltpu.make_async_copy(dark_h, dark, sem.at[CHUNKS + 1]),
-        pltpu.make_async_copy(counts_h, counts, sem.at[CHUNKS + 2]),
+        pltpu.make_async_copy(counts_h, counts, sem.at[CHUNKS]),
+        pltpu.make_async_copy(basis_h, basis, sem.at[CHUNKS + 1]),
+        pltpu.make_async_copy(dark_h, dark, sem.at[CHUNKS + 2]),
     ]
     large = []
     for c in range(CHUNKS):
@@ -62,10 +63,10 @@
         large.append(pltpu.make_async_copy(raw_h.at[t], raw.at[t], sem.at[c]))
     for copy in small + large:
         copy.start()
-    for copy in small:
-        copy.wait()
+    small[1].wait()
     weights = jnp.concatenate([basis[...], jnp.ones((rank, pixels), jnp.bfloat16)], axis=0)
     contract = (((1,), (1,)), ((), ()))
+    small[2].wait()
     dark_rows = lax.dot_general(
         dark[...], weights, contract, preferred_element_type=jnp.float32
     )
@@ -74,20 +75,25 @@
     acc = jnp.zeros((planes, 2 * rank), jnp.float32)
     ends = [slice((r + 1) * COLS - OVL, (r + 1) * COLS) for r in range(ROWS)]
     dark_ends = [dark[:, x].astype(jnp.float32) for x in ends]
+    rows = []
     for c in range(CHUNKS):
+        if c == CHUNKS - 1:
+            small[0].wait()
+            for t in range(tiles):
+                limits[t] = jnp.full(limits.shape[1:], counts[t], jnp.int32)
         large[c].wait()
-        t0 = c * chunk
-        rows = lax.dot_general(
-            raw[t0 : t0 + chunk].reshape(chunk * planes, pixels), weights, contract,
-            preferred_element_type=jnp.float32,
-        ).reshape(chunk, planes, 2 * rank)
-        for i in range(chunk):
-            t = t0 + i
-            acc = acc + jnp.where(plane < counts[t], rows[i] - dark_rows, 0.0)
-            for r in range(ROWS):
-                value = raw[t, :, ends[r]].astype(jnp.float32)
-                kept = jnp.where(wide_plane < counts[t], value, dark_ends[r])
-                edges[t, :, r * OVL : (r + 1) * OVL] = kept.astype(jnp.bfloat16)
+        rows.append(
+            lax.dot_general(
+                raw[c * chunk : (c + 1) * chunk].reshape(chunk * planes, pixels), weights,
+                contract, preferred_element_type=jnp.float32,
+            ).reshape(chunk, planes, 2 * rank)
+        )
+    for t in range(tiles):
+        acc = acc + jnp.where(plane < counts[t], rows[t // chunk][t % chunk] - dark_rows, 0.0)
+        for r in range(ROWS):
+            value = raw[t, :, ends[r]].astype(jnp.float32)
+            kept = jnp.where(wide_plane < counts[t], value, dark_ends[r])
+            edges[t, :, r * OVL : (r + 1) * OVL] = kept.astype(jnp.bfloat16)
     pad = jnp.zeros((planes, LANES - 2 * rank), jnp.float32)
     rows = packed(jnp.concatenate([acc, pad], axis=1))
     out[...] = jnp.broadcast_to(rows[None], out.shape)
@@ -99,8 +105,10 @@
     hit = row // 2 == col
     up = (row.astype(jnp.float32) + 0.5) / OVL
     down = (WIDE - row.astype(jnp.float32) - 0.5) / OVL
+
     def of(scale):
         return jnp.where(hit, 0.25 * jnp.minimum(1.0, scale), 0.0).astype(jnp.bfloat16)
+
     return of(up), of(jnp.ones_like(up)), of(down)
 
 
@@ -111,22 +119,27 @@
     return jnp.where(row // 2 == col, 0.25 * scale, 0.0).astype(jnp.bfloat16)
 
 
-def correct_kernel(
-    counts_h, positions_h, parts, raw, dark, basis, edges, corrected_h, cells_h,
-    corrected, cells, inverse, counts, positions, sem,
-):
-    tiles, planes, pixels = raw.shape
+def block_cells(j, weight, raw, dark, inverse, limits, corrected):
+    tiles, planes, _ = raw.shape
+    plane = lax.broadcasted_iota(jnp.int32, (planes, WIDE), 0)
+    acc = None
+    for r in range(ROWS):
+        x = slice(r * COLS + j * WIDE, r * COLS + (j + 1) * WIDE)
+        scale = inverse[:, x]
+        dark_f = dark[:, x].astype(jnp.float32)
+        for t in range(tiles):
+            value = (raw[t, :, x].astype(jnp.float32) - dark_f) * scale
+            corrected[t, :, x] = jnp.where(plane < limits[t], value, 0.0).astype(jnp.bfloat16)
+        part = jnp.dot(
+            corrected[:, :, x].reshape(tiles * planes, WIDE), weight,
+            preferred_element_type=jnp.float32,
+        )
+        acc = part if acc is None else acc + part
+    return acc.astype(jnp.bfloat16).reshape(tiles, planes, LANES)
+
+
+def fill_inverse(parts, basis, inverse):
     rank = basis.shape[0]
-    half = planes // 2
-    copies = [
-        pltpu.make_async_copy(counts_h, counts, sem.at[0]),
-        pltpu.make_async_copy(positions_h, positions, sem.at[1]),
-    ]
-    for copy in copies:
-        copy.start()
-    columns = lax.axis_size(DEV)
-    own = (lax.axis_index(GRP) * columns + lax.axis_index(DEV)) * tiles
-    before = jnp.maximum(own - tiles, 0)
     terms = unpacked(jnp.sum(parts[...], axis=0))
     coef = (terms / pltpu.roll(terms, LANES - rank, 1))[:, :rank]
     high = coef.astype(jnp.bfloat16)
@@ -139,13 +152,11 @@
         coef3, jnp.concatenate([base, base, base], axis=0), preferred_element_type=jnp.float32
     )
     inverse[...] = jnp.exp(-shade)
-    leaving = []
-
-    def leave(source, target):
-        copy = pltpu.make_async_copy(source, target, sem.at[2 + len(leaving)])
-        copy.start()
-        leaving.append(copy)
-
+
+
+def store_tails(edges, dark, inverse, tails):
+    tiles, planes, _ = edges.shape
+    half = planes // 2
     ends = [slice((r + 1) * COLS - OVL, (r + 1) * COLS) for r in range(ROWS)]
     value = jnp.concatenate(
         [
@@ -155,50 +166,68 @@
         ],
         axis=2,
     )
-    tails = jnp.dot(
+    sums = jnp.dot(
         value.reshape(tiles * planes, ROWS * OVL), tail_weights(),
         preferred_element_type=jnp.float32,
     ).reshape(tiles, planes, LANES)
     left = lax.broadcasted_iota(jnp.int32, (half, LANES), 1) < HALF
-    for copy in copies:
-        copy.wait()
     for t in range(tiles):
-        band = positions[before + t] // (columns * tiles)
-        joined = jnp.where(left, tails[t, :half], tails[t, half:])
-        cells[band, COLS // WIDE * planes :, :] = joined.astype(jnp.bfloat16)
-    plane = lax.broadcasted_iota(jnp.int32, (planes, WIDE), 0)
+        tails[t] = jnp.where(left, sums[t, :half], sums[t, half:]).astype(jnp.bfloat16)
+
+
+def correct_kernel(
+    positions_h, parts, raw, dark, basis, edges, limits, corrected, cells_h,
+    cells, tails, early, inverse, positions, sem,
+):
+    tiles, planes, _ = raw.shape
+    half = planes // 2
+    blocks = COLS // WIDE
+    band_size = lax.axis_size(DEV) * tiles
+    fetch = pltpu.make_async_copy(positions_h, positions, sem.at[blocks])
+    fetch.start()
+    own = (lax.axis_index(GRP) * lax.axis_size(DEV) + lax.axis_index(DEV)) * tiles
+    before = jnp.maximum(own - tiles, 0)
+    fill_inverse(parts, basis, inverse)
+    store_tails(edges, dark, inverse, tails)
     first, inner, last = pair_weights()
-    blocks = COLS // WIDE
+    leaving = []
+
+    def leave(x, slot):
+        copy = pltpu.make_async_copy(cells.at[:, x, :], cells_h.at[:, x, :], sem.at[slot])
+        copy.start()
+        leaving.append(copy)
+
     for j in range(blocks):
         weight = first if j == 0 else last if j == blocks - 1 else inner
-        acc = None
-        for r in range(ROWS):
-            x = slice(r * COLS + j * WIDE, r * COLS + (j + 1) * WIDE)
-            scale = inverse[:, x]
-            dark_f = dark[:, x].astype(jnp.float32)
+        pooled = block_cells(j, weight, raw, dark, inverse, limits, corrected)
+        if j < EARLY:
+            early[j] = pooled
+            continue
+        if j == EARLY:
+            fetch.wait()
+            bands = [positions[own + t] // band_size for t in range(tiles)]
             for t in range(tiles):
-                value = (raw[t, :, x].astype(jnp.float32) - dark_f) * scale
-                corrected[t, :, x] = jnp.where(plane < counts[t], value, 0.0).astype(jnp.bfloat16)
-            leave(corrected.at[:, :, x], corrected_h.at[:, :, x])
-            part = jnp.dot(
-                corrected[:, :, x].reshape(tiles * planes, WIDE), weight,
-                preferred_element_type=jnp.float32,
-            )
-            acc = part if acc is None else acc + part
-        pooled = acc.astype(jnp.bfloat16).reshape(tiles, planes, LANES)
+                cells[positions[before + t] // band_size, blocks * planes :, :] = tails[t]
+                for i in range(EARLY):
+                    cells[bands[t], i * planes : (i + 1) * planes, :] = early[i, t]
+            leave(slice(blocks * planes, blocks * planes + half), 0)
+            leave(slice(0, EARLY * planes), 1)
         for t in range(tiles):
-            band = positions[own + t] // (columns * tiles)
-            cells[band, j * planes : (j + 1) * planes, :] = pooled[t]
-        x = slice(j * planes, (j + 1) * planes + (half if j == blocks - 1 else 0))
-        leave(cells.at[:, x, :], cells_h.at[:, x, :])
+            cells[bands[t], j * planes : (j + 1) * planes, :] = pooled[t]
+        leave(slice(j * planes, (j + 1) * planes), j)
     for copy in leaving:
         copy.wait()
+
+
+def flush_kernel(held, out_h, sem):
+    copy = pltpu.make_async_copy(held, out_h, sem)
+    copy.start()
+    copy.wait()
 
 
 def stitch_kernel(sources, arrived, out_h, out, sem):
     planes = out.shape[0]
     count = arrived.shape[0]
-    half = planes // 2
     blocks = COLS // 2 // LANES
     step = (COLS - OVL) // 2
     lane = lax.broadcasted_iota(jnp.int32, (planes, LANES), 1)
@@ -266,24 +295,25 @@
 
 
 def per_device(raw, dark, basis, counts, positions):
-    tiles, planes, pixels = raw.shape
+    tiles, planes, _ = raw.shape
     groups = lax.axis_size(GRP)
     columns = lax.axis_size(DEV)
     width = COLS // 2
     span = tiles * (COLS - OVL) // 2
     height = width // LANES * planes + planes // 2
     first, second = lax.axis_size(FIRST), lax.axis_size(SECOND)
-    terms, raw_v, dark_v, basis_v, edges = pl.pallas_call(
+    terms, raw_v, dark_v, basis_v, edges, limits = pl.pallas_call(
         terms_kernel,
         out_shape=(
-            pltpu.VMEM((first, planes // SUBLANES, LANES), jnp.float32),
+            jax.ShapeDtypeStruct((first, planes // SUBLANES, LANES), jnp.float32),
             pltpu.VMEM(raw.shape, jnp.bfloat16),
             pltpu.VMEM(dark.shape, jnp.bfloat16),
             pltpu.VMEM(basis.shape, jnp.bfloat16),
             jax.ShapeDtypeStruct((tiles, planes, ROWS * OVL), jnp.bfloat16),
+            pltpu.VMEM((tiles, planes, WIDE), jnp.int32),
         ),
         in_specs=[HBM, HBM, HBM, HBM],
-        out_specs=(VMEM, VMEM, VMEM, VMEM, VMEM),
+        out_specs=(VMEM,) * 6,
         scratch_shapes=[
             pltpu.SMEM((tiles,), jnp.int32),
             pltpu.SemaphoreType.DMA((CHUNKS + 3,)),
@@ -291,10 +321,11 @@
         compiler_params=LIMIT,
         name="terms",
     )(in_hbm(counts), in_hbm(raw), in_hbm(dark), in_hbm(basis))
-    once = jnp.sum(exchanged(terms, FIRST), axis=0)
-    edges, positions_late, once = lax.optimization_barrier((edges, positions, once))
+    column_sums = exchanged(terms, FIRST)
+    edges = lax.ppermute(edges, DEV, [(d, d + 1) for d in range(columns - 1)])
+    once = jnp.sum(column_sums, axis=0)
     parts = exchanged(jnp.broadcast_to(once[None], (second, *once.shape)), SECOND)
-    edges = lax.ppermute(edges, DEV, [(d, d + 1) for d in range(columns - 1)])
+    positions_late, parts = lax.optimization_barrier((positions, parts))
     here_dev = lax.axis_index(DEV)
     own_sources = sources_of(positions_late, here_dev, groups, columns, tiles)
     left_dev = jnp.maximum(here_dev - 1, 0)
@@ -303,26 +334,36 @@
     corrected, outgoing = pl.pallas_call(
         correct_kernel,
         out_shape=(
-            jax.ShapeDtypeStruct(raw.shape, jnp.bfloat16),
+            pltpu.VMEM(raw.shape, jnp.bfloat16),
             jax.ShapeDtypeStruct((groups, height, LANES), jnp.bfloat16),
         ),
-        in_specs=[HBM, HBM, VMEM, VMEM, VMEM, VMEM, VMEM],
-        out_specs=(HBM, HBM),
+        in_specs=[HBM] + [VMEM] * 6,
+        out_specs=(VMEM, HBM),
         scratch_shapes=[
-            pltpu.VMEM(raw.shape, jnp.bfloat16),
             pltpu.VMEM((groups, height, LANES), jnp.bfloat16),
+            pltpu.VMEM((tiles, planes // 2, LANES), jnp.bfloat16),
+            pltpu.VMEM((EARLY, tiles, planes, LANES), jnp.bfloat16),
             pltpu.VMEM(dark.shape, jnp.float32),
-            pltpu.SMEM((tiles,), jnp.int32),
             pltpu.SMEM(positions.shape, jnp.int32),
-            pltpu.SemaphoreType.DMA((2 + pixels // WIDE + width // LANES,)),
+            pltpu.SemaphoreType.DMA((COLS // WIDE + 1,)),
         ],
+        input_output_aliases={2: 0},
         compiler_params=LIMIT,
         name="correct",
     )(
-        in_hbm(counts), in_hbm(positions), in_vmem(parts), in_vmem(raw_v), in_vmem(dark_v),
-        in_vmem(basis_v), in_vmem(edges),
+        in_hbm(positions), in_vmem(parts), in_vmem(raw_v), in_vmem(dark_v), in_vmem(basis_v),
+        in_vmem(edges), in_vmem(limits),
     )
     arrived = exchanged(outgoing, GRP)
+    flushed = pl.pallas_call(
+        flush_kernel,
+        out_shape=jax.ShapeDtypeStruct(raw.shape, jnp.bfloat16),
+        in_specs=[VMEM],
+        out_specs=HBM,
+        scratch_shapes=[pltpu.SemaphoreType.DMA],
+        compiler_params=LIMIT,
+        name="flush",
+    )(in_vmem(corrected))
     pooled = pl.pallas_call(
         stitch_kernel,
         out_shape=jax.ShapeDtypeStruct((planes, span), jnp.bfloat16),
@@ -335,7 +376,7 @@
         compiler_params=LIMIT,
         name="stitch",
     )(sources, in_vmem(arrived))
-    return corrected, pooled.reshape(1, planes, ROWS // 2, span)
+    return flushed, pooled.reshape(1, planes, ROWS // 2, span)
 
 
 def solution(mesh):

time: 70.9 us -> 71.4 us (level)
  the two profiles are of different devices: /device:TPU:1 before, /device:TPU:8 now
where the time goes in v3:
time: 71.4 us; the launch traced here: 71.1 us
  blocking collectives  37.8 us (53%)
  waiting for transfers between devices  16 us (22%)
  Pallas kernels  9.16 us (13%)
  starting transfers between devices  5.51 us (8%)
  other arithmetic  1.11 us (2%)
  local copies, waits for them, and re-layouts  0.76 us (1%)
  between operations  0.72 us (1%)
    all_to_all x2, blocking collectives, exchanged(): return lax.all_to_all(copies, axes, split_axis=0, concat_axis=0, tiled=True)  37.8 us
    all_to_all x1, waiting for transfers between devices, exchanged(): return lax.all_to_all(copies, axes, split_axis=0, concat_axis=0, tiled=True)  16 us
    all_to_all x1, starting transfers between devices, exchanged(): return lax.all_to_all(copies, axes, split_axis=0, concat_axis=0, tiled=True)  3.59 us
    pallas_call x1, Pallas kernels, per_device(): pl.pallas_call(correct_kernel, out_shape=(pltpu.VMEM(raw.shape, jnp.bfloa...  3.36 us
    pallas_call x1, Pallas kernels, per_device(): pl.pallas_call(terms_kernel, out_shape=(jax.ShapeDtypeStruct((first, plan...  3.01 us
    ppermute x1, starting transfers between devices, per_device(): edges = lax.ppermute(edges, DEV, [(d, d + 1) for d in range(columns - 1)])  1.92 us
    pallas_call x1, Pallas kernels, per_device(): pl.pallas_call(stitch_kernel, out_shape=jax.ShapeDtypeStruct((planes, spa...  1.47 us
  transfers between devices with their start and end apart: 2, of which 1 were waited for; matrix products, arithmetic and copies ran while one was open for 3% of the time, Pallas kernels for 2%

profile of v3, /device:TPU:8, one launch (start us, length us, event | category | flops | bytes accessed | tf_op | source)
XLA Modules:
  0.0 71.1 jit_solution(10733571417125552752)
XLA Ops:
  0.6 3.0 %terms.1 = (f32[16,2,128]{2,1,0:T(2,128)S(1)}, bf16[16,16,4096]{2,1,0:T(8,128)(2,1)S(1)}, bf16[16,4096]{1,0:T(8,128)(2,1)S(1)}, bf16[8,4096]{1,0:T(8,128)(2,1)S(...) custom-call(s32[16]{0:T(128)} %counts_h.1, bf16[16,16,4096]{2,1,0:T(8,128)(2,1)} %raw_h.1, ...), custom_call_target="tpu_custom_call" | custom-call | tf_op jit(solution)/shard_map/terms/pallas_call | solution.py:305
  3.6 0.0 copy-start
  3.7 1.9 %collective-permute-start = (bf16[16,16,256]{2,1,0:T(8,128)(2,1)S(1)}, bf16[16,16,256]{2,1,0:T(8,128)(2,1)S(1)}, u32[]{:S(2)}, u32[]{:S(2)}) collective-permute-start(bf16[16,16,256]{2,1,0:T(8,128)(2,1)S(1)} %get-tuple-element.17), channel_id=1, source_target_pairs={{0,1},{1,2},{2,3},{3,4},{4,5},{5,6},{6,7},{7,8},{8,9},{9,10},{10,1... | collective-permute-start | bytes 393224 | tf_op jit(solution)/shard_map/ppermute | solution.py:325
  5.6 19.0 %all_to_all.15 = f32[16,2,128]{2,1,0:T(2,128)S(1)} all-to-all(f32[16,2,128]{2,1,0:T(2,128)S(1)} %get-tuple-element.12), channel_id=1, replica_groups=mesh['grp_0'=4,'grp_1'=4,'dev_0'=2,'dev_1'=8,'dev_2'=2] {'dev_1','dev_2'}, dimensions={0} | all-to-all | bytes 32768 | tf_op jit(solution)/shard_map/all_to_all | solution.py:284
  24.7 18.8 %all_to_all.16.parts = f32[32,2,128]{2,1,0:T(2,128)S(1)} all-to-all(f32[32,2,128]{2,1,0:T(2,128)S(1)} %broadcast_in_dim.31), channel_id=1, replica_groups=mesh['grp_0'=4,'grp_1'=4,'dev_0'=2,'dev_1'=8,'dev_2'=2] {'grp_0','grp_1'..., dimensions={0} | all-to-all | bytes 65536 | tf_op jit(solution)/shard_map/all_to_all | solution.py:284
  43.4 0.0 collective-permute-done.edges
  43.5 3.4 %correct.1 = (bf16[16,16,4096]{2,1,0:T(8,128)(2,1)S(1)}, bf16[16,136,128]{2,1,0:T(8,128)(2,1)}) custom-call(s32[8192]{0:T(1024)} %positions_h.1, f32[32,2,128]{2,1,0:T(2,128)S(1)} %all_to_all.16.parts, bf16[16,16,4096]{2,1,0:T(8,128)(2,1)S(1)} %get-tuple-element.14.raw, ...), custom_call_target="tpu_custom_call", output_to_operand_aliasing={{0}: (2, {})} | custom-call | tf_op jit(solution)/shard_map/correct/pallas_call | solution.py:334
  46.8 3.6 %all-to-all-start.2 = ((bf16[16,136,128]{2,1,0:T(8,128)(2,1)}), bf16[16,136,128]{2,1,0:T(8,128)(2,1)S(1)}, u32[]{:S(2)}, u32[]{:S(2)}) async-start(bf16[16,136,128]{2,1,0:T(8,128)(2,1)} %get-tuple-element.21), calls=%async_computation.2 | async-start | bytes 1114112 | tf_op jit(solution)/shard_map/all_to_all | solution.py:284
  50.4 0.0 copy-done
  50.4 0.1 reshape.14
  50.6 0.1 fusion.3
  50.7 0.1 select_reduce_fusion
  50.9 0.6 slice.3
  51.4 0.1 select_reduce_fusion.1
  51.6 0.7 %pad_add_fusion.sources = s32[17]{0:T(128)S(1)} fusion(s32[1]{0:T(128)} %slice.3, s32[16]{0:T(128)S(1)} %select_reduce_fusion.1), kind=kLoop, calls=%fused_computation.30 | loop fusion | flops 17 | bytes 136 | tf_op jit(solution)/shard_map/concatenate | solution.py:333
  52.3 1.3 %flush.1 = bf16[16,16,4096]{2,1,0:T(8,128)(2,1)} custom-call(bf16[16,16,4096]{2,1,0:T(8,128)(2,1)S(1)} %get-tuple-element.19.held), custom_call_target="tpu_custom_call" | custom-call | tf_op jit(solution)/shard_map/flush/pallas_call | solution.py:358
  53.6 16.0 %all-to-all-done.2.arrived = bf16[16,136,128]{2,1,0:T(8,128)(2,1)S(1)} async-done(((bf16[16,136,128]{2,1,0:T(8,128)(2,1)}), bf16[16,136,128]{2,1,0:T(8,128)(2,1)S(1)}, u32[]{:S(2)}, u32[]{:S(2)}) %all-to-all-start.2) | async-done | bytes 557088 | tf_op jit(solution)/shard_map/all_to_all | solution.py:284
  69.6 1.5 %stitch.1 = bf16[16,15360]{1,0:T(8,128)(2,1)} custom-call(s32[17]{0:T(128)S(1)} %pad_add_fusion.sources, bf16[16,136,128]{2,1,0:T(8,128)(2,1)S(1)} %all-to-all-done.2.arrived), custom_call_target="tpu_custom_call" | custom-call | tf_op jit(solution)/shard_map/stitch/pallas_call | solution.py:367
  (3 shorter events, 0.1 us)
Async XLA Ops:
  3.6 46.8 %copy-start = (s32[8192]{0:T(1024)S(1)}, s32[8192]{0:T(1024)}, u32[]{:S(2)}) copy-start(s32[8192]{0:T(1024)} %positions_h.1) | copy-start | bytes 98308
  3.7 39.8 %collective-permute-start = (bf16[16,16,256]{2,1,0:T(8,128)(2,1)S(1)}, bf16[16,16,256]{2,1,0:T(8,128)(2,1)S(1)}, u32[]{:S(2)}, u32[]{:S(2)}) collective-permute-start(bf16[16,16,256]{2,1,0:T(8,128)(2,1)S(1)} %get-tuple-element.17), channel_id=1, source_target_pairs={{0,1},{1,2},{2,3},{3,4},{4,5},{5,6},{6,7},{7,8},{8,9},{9,10},{10,1... | collective-permute-start | bytes 393224 | tf_op jit(solution)/shard_map/ppermute | solution.py:325
  46.8 22.8 %all-to-all-start.2 = ((bf16[16,136,128]{2,1,0:T(8,128)(2,1)}), bf16[16,136,128]{2,1,0:T(8,128)(2,1)S(1)}, u32[]{:S(2)}, u32[]{:S(2)}) async-start(bf16[16,136,128]{2,1,0:T(8,128)(2,1)} %get-tuple-element.21), calls=%async_computation.2 | async-start | bytes 1114112 | tf_op jit(solution)/shard_map/all_to_all | solution.py:284
